TPU v7x, 32 devices: a whole 2x2x4 slice. The times are simulated.
32 devices in a mesh: gx: 4 (over x, core), gy: 8 (over z, y).
Axes of the slice: x: 2, y: 2, z: 4, core: 2. Of those that a mesh axis runs over, the one named last changes fastest.
Arguments:
- populations: float32 [19, 32, 64, 128], P(None, 'gx', 'gy'), may hold values from 0 to 1, as said below
- cell_kind: int32 [32, 64, 128], P('gx', 'gy'), may hold values from 0 to 3, as said below
- outlet_region: int32 [32, 64], P('gx', 'gy'), may hold values from 0 to 63, as said below
Outputs:
- final_populations: float32 [19, 32, 64, 128], P(None, 'gx', 'gy')
- outlet_means: float32 [2, 64], replicated
Inputs may be any that keep to these rules, and one draw needn't show every extreme that they name: `populations`: positive. `cell_kind`: the plane z = 0 is all inlet (2), the plane z = 127 all outlet (3); all other cells are fluid (0) or wall (1). `outlet_region`: every region names at least one column; ids are constant on aligned tiles of 4 x 4 columns.
All inputs are finite; a program needn't handle non-finite values.
Results may differ from a plain program's by a relative error of at most 0.0001.
Values sent between devices are 32-bit elements; how exact they have to be, the bound alone decides.
A program may use at most 64 MiB of HBM per device.

v0:
```python
import jax
import jax.numpy as jnp
from jax import lax
from jax.sharding import PartitionSpec as P

REGIONS = 64
STEPS = 2
VELOCITIES = (
    (0, 0, 0),
    (1, 0, 0),
    (-1, 0, 0),
    (0, 1, 0),
    (0, -1, 0),
    (0, 0, 1),
    (0, 0, -1),
    (1, 1, 0),
    (-1, -1, 0),
    (1, -1, 0),
    (-1, 1, 0),
    (1, 0, 1),
    (-1, 0, -1),
    (1, 0, -1),
    (-1, 0, 1),
    (0, 1, 1),
    (0, -1, -1),
    (0, 1, -1),
    (0, -1, 1),
)
WEIGHTS = (1.0 / 3.0,) + (1.0 / 18.0,) * 6 + (1.0 / 36.0,) * 12
OPPOSITE = (0, 2, 1, 4, 3, 6, 5, 8, 7, 10, 9, 12, 11, 14, 13, 16, 15, 18, 17)
RELAX_TIME = 0.8
INLET_SPEED = 0.05
RISING_X = (1, 7, 9, 11, 13)
FALLING_X = (2, 8, 10, 12, 14)
RISING_Y = (3, 7, 10, 15, 17)
FALLING_Y = (4, 8, 9, 16, 18)


def from_behind(block, axis, distance):
    devices = range(lax.axis_size(axis))
    route = [(i - distance, i) for i in devices if i - distance in devices]
    return lax.ppermute(block, axis, route)


def from_behind_2(value, axis, steps):
    count = lax.axis_size(axis)
    pairs = [(source, (source + steps) % count) for source in range(count)]
    return lax.ppermute(value, axis, pairs)


def momentum(current, direction):
    total = jnp.zeros_like(current[0])
    for number in range(19):
        factor = VELOCITIES[number][direction]
        if factor != 0:
            total = total + factor * current[number]
    return total


def equilibrium(density, vel_x, vel_y, vel_z):
    speed_sq = vel_x * vel_x + vel_y * vel_y + vel_z * vel_z
    result = []
    for number in range(19):
        comp_x, comp_y, comp_z = VELOCITIES[number]
        projected = comp_x * vel_x + comp_y * vel_y + comp_z * vel_z
        result.append(
            WEIGHTS[number]
            * density
            * (1.0 + 3.0 * projected + 4.5 * projected * projected - 1.5 * speed_sq)
        )
    return jnp.stack(result)


def collide(current, kinds, col_mean):
    density = jnp.sum(current, axis=0)
    vel_x = momentum(current, 0) / density
    vel_y = momentum(current, 1) / density
    vel_z = momentum(current, 2) / density
    relaxed = current - (current - equilibrium(density, vel_x, vel_y, vel_z)) / RELAX_TIME
    bounced = jnp.stack([current[OPPOSITE[number]] for number in range(19)])
    unity = jnp.ones_like(density)
    still = jnp.zeros_like(density)
    inlet = equilibrium(unity, still, still, INLET_SPEED * unity)
    outlet = equilibrium(col_mean * unity, vel_x, vel_y, vel_z)
    post = jnp.where(kinds == 1, bounced, relaxed)
    post = jnp.where(kinds == 2, inlet, post)
    post = jnp.where(kinds == 3, outlet, post)
    return post


def stream(padded, rows_x, rows_y):
    moved = []
    for number in range(19):
        comp_x, comp_y, comp_z = VELOCITIES[number]
        plane = padded[
            number, 1 - comp_x : 1 - comp_x + rows_x, 1 - comp_y : 1 - comp_y + rows_y, :
        ]
        moved.append(jnp.roll(plane, comp_z, axis=2))
    return jnp.stack(moved)


def outlet_mean(current, kinds, onehot):
    density = jnp.sum(current, axis=0)
    is_outlet = kinds == 3
    column = jnp.sum(jnp.where(is_outlet, density, 0.0), axis=2).reshape(-1)
    col_count = jnp.sum(is_outlet.astype(jnp.float32), axis=2).reshape(-1)
    local_sums = jnp.dot(onehot, column, precision=lax.Precision.HIGHEST)
    local_counts = jnp.dot(onehot, col_count, precision=lax.Precision.HIGHEST)
    totals, counts = lax.psum((local_sums, local_counts), ("gx", "gy"))
    return totals / counts


def widen_first(post, from_lower, from_upper):
    blank = jnp.zeros_like(post[0, :1])
    planes = []
    for number in range(19):
        lower = from_lower[RISING_X.index(number)][None] if number in RISING_X else blank
        upper = from_upper[FALLING_X.index(number)][None] if number in FALLING_X else blank
        planes.append(jnp.concatenate([lower, post[number], upper], axis=0))
    return planes


def widen_second(planes, from_lower, from_upper):
    blank = jnp.zeros_like(planes[0][:, :1])
    padded = []
    for number in range(19):
        lower = from_lower[RISING_Y.index(number)][:, None] if number in RISING_Y else blank
        upper = from_upper[FALLING_Y.index(number)][:, None] if number in FALLING_Y else blank
        padded.append(jnp.concatenate([lower, planes[number], upper], axis=1))
    return jnp.stack(padded)


def body(populations, cell_kind, outlet_region):
    cells_x = populations.shape[1]
    cells_y = populations.shape[2]
    labels = jnp.arange(REGIONS, dtype=jnp.int32)
    onehot = (outlet_region.reshape(-1)[None, :] == labels[:, None]).astype(jnp.float32)
    current = populations
    means = []
    for timestep in range(STEPS):
        region_mean = outlet_mean(current, cell_kind, onehot)
        means.append(region_mean)
        col_mean = jnp.dot(region_mean, onehot, precision=lax.Precision.HIGHEST).reshape(
            cells_x, cells_y
        )[:, :, None]
        post = collide(current, cell_kind, col_mean)
        lower_x = from_behind(jnp.stack([post[number, -1] for number in RISING_X]), "gx", 1)
        upper_x = from_behind(jnp.stack([post[number, 0] for number in FALLING_X]), "gx", -1)
        planes = widen_first(post, lower_x, upper_x)
        lower_y = from_behind_2(jnp.stack([planes[number][:, -1] for number in RISING_Y]), "gy", 1)
        upper_y = from_behind_2(jnp.stack([planes[number][:, 0] for number in FALLING_Y]), "gy", -1)
        padded = widen_second(planes, lower_y, upper_y)
        current = stream(padded, cells_x, cells_y)
    return (current, jnp.stack(means))


def solution(mesh):
    in_specs = (P(None, "gx", "gy", None), P("gx", "gy", None), P("gx", "gy"))
    out_specs = (P(None, "gx", "gy", None), P())
    return jax.shard_map(body, mesh=mesh, in_specs=in_specs, out_specs=out_specs, check_vma=False)
```

profile of v0, /device:TPU:1, one launch (start us, length us, event | category | flops | bytes accessed | tf_op | source)
XLA Modules:
  0.0 127.7 jit_solution(15017054482665278097)
XLA Ops:
  0.7 0.8 constant_dynamic-update-slice_fusion.47
  1.5 1.1 reduce_sum.854
  2.6 0.1 constant_dynamic-update-slice_fusion.66
  2.7 0.7 copy-done.1
  3.4 0.1 convert_reduce_fusion
  4.1 0.6 copy-done.2
  4.8 0.1 convolution_bitcast_fusion.3
  4.9 0.2 convolution_bitcast_fusion.4
  5.1 40.5 %all-reduce = (f32[64]{0:T(128)S(1)}, f32[64]{0:T(128)S(1)}) all-reduce(f32[64]{0:T(128)S(1)} %convolution_bitcast_fusion.4, f32[64]{0:T(128)S(1)} %convolution_bitcast_fusion.3), channel_id=1, replica_groups=mesh['gx'=4,'gy'=8] {'gx','gy'}, use_global_device_ids=true, to_apply=%region_2.3 | all-reduce | flops 128 | bytes 1024 | tf_op jit(solution)/shard_map/psum | solution.py:109
  45.6 0.1 broadcast_multiply_fusion.2
  47.8 0.3 select_select_fusion.1
  48.2 5.3 %collective-permute-start = (f32[5,8,128]{2,1,0:T(8,128)S(1)}, f32[5,8,128]{2,1,0:T(8,128)S(1)}, u32[]{:S(2)}, u32[]{:S(2)}) collective-permute-start(f32[5,8,128]{2,1,0:T(8,128)S(1)} %get-tuple-element.153), channel_id=1, source_target_pairs={{0,8},{8,16},{16,24},{1,9},{9,17},{17,25},{2,10},{10,18},{18,26},{... | collective-permute-start | bytes 61448 | tf_op jit(solution)/shard_map/ppermute | solution.py:42
  53.5 1.9 %collective-permute-start.1 = (f32[5,8,128]{2,1,0:T(8,128)S(1)}, f32[5,8,128]{2,1,0:T(8,128)S(1)}, u32[]{:S(2)}, u32[]{:S(2)}) collective-permute-start(f32[5,8,128]{2,1,0:T(8,128)S(1)} %get-tuple-element.154), channel_id=1, source_target_pairs={{8,0},{16,8},{24,16},{9,1},{17,9},{25,17},{10,2},{18,10},{26,18},{... | collective-permute-start | bytes 61448 | tf_op jit(solution)/shard_map/ppermute | solution.py:42
  55.5 3.1 %collective-permute-done.1 = f32[5,8,128]{2,1,0:T(8,128)S(1)} collective-permute-done((f32[5,8,128]{2,1,0:T(8,128)S(1)}, f32[5,8,128]{2,1,0:T(8,128)S(1)}, u32[]{:S(2)}, u32[]{:S(2)}) %collective-permute-start.1) | collective-permute-done | bytes 20512 | tf_op jit(solution)/shard_map/ppermute | solution.py:42
  58.7 0.3 collective-permute-start.2
  59.2 4.0 %collective-permute-start.3 = (f32[5,10,128]{2,0,1:T(8,128)S(1)}, f32[5,10,128]{2,0,1:T(8,128)S(1)}, u32[]{:S(2)}, u32[]{:S(2)}) collective-permute-start(f32[5,10,128]{2,0,1:T(8,128)S(1)} %stack.147), channel_id=1, source_target_pairs={{0,7},{1,0},{2,1},{3,2},{4,3},{5,4},{6,5},{7,6},{8,15},{9,8},{10,9... | collective-permute-start | bytes 76808 | tf_op jit(solution)/shard_map/ppermute | solution.py:48
  63.2 1.1 collective-permute-done.2
  65.7 0.3 constant_dynamic-update-slice_fusion.152
  66.8 0.1 fusion.168
  67.0 0.1 convolution_bitcast_fusion.1
  67.2 38.7 %psum.26 = f32[64]{0:T(128)S(1)} all-reduce(f32[64]{0:T(128)S(1)} %convolution_bitcast_fusion.1), channel_id=1, replica_groups=mesh['gx'=4,'gy'=8] {'gx','gy'}, use_global_device_ids=true, to_apply=%region_6.7 | all-reduce | flops 64 | bytes 512 | tf_op jit(solution)/shard_map/psum | solution.py:109
  105.9 0.1 broadcast_multiply_fusion.1
  106.3 0.1 constant_dynamic-update-slice_fusion.94
  107.7 0.3 select_select_fusion
  108.2 5.3 %collective-permute-start.4 = (f32[5,8,128]{2,1,0:T(8,128)S(1)}, f32[5,8,128]{2,1,0:T(8,128)S(1)}, u32[]{:S(2)}, u32[]{:S(2)}) collective-permute-start(f32[5,8,128]{2,1,0:T(8,128)S(1)} %get-tuple-element.125), channel_id=1, source_target_pairs={{0,8},{8,16},{16,24},{1,9},{9,17},{17,25},{2,10},{10,18},{18,26},{... | collective-permute-start | bytes 61448 | tf_op jit(solution)/shard_map/ppermute | solution.py:42
  113.4 1.9 %collective-permute-start.5 = (f32[5,8,128]{2,1,0:T(8,128)S(1)}, f32[5,8,128]{2,1,0:T(8,128)S(1)}, u32[]{:S(2)}, u32[]{:S(2)}) collective-permute-start(f32[5,8,128]{2,1,0:T(8,128)S(1)} %get-tuple-element.124), channel_id=1, source_target_pairs={{8,0},{16,8},{24,16},{9,1},{17,9},{25,17},{10,2},{18,10},{26,18},{... | collective-permute-start | bytes 61448 | tf_op jit(solution)/shard_map/ppermute | solution.py:42
  115.4 0.6 pad_maximum_fusion.164
  116.0 2.6 %collective-permute-done.5 = f32[5,8,128]{2,1,0:T(8,128)S(1)} collective-permute-done((f32[5,8,128]{2,1,0:T(8,128)S(1)}, f32[5,8,128]{2,1,0:T(8,128)S(1)}, u32[]{:S(2)}, u32[]{:S(2)}) %collective-permute-start.5) | collective-permute-done | bytes 20512 | tf_op jit(solution)/shard_map/ppermute | solution.py:42
  118.7 0.8 collective-permute-start.7
  119.5 0.7 collective-permute-start.6
  120.7 4.5 %collective-permute-done.6 = f32[5,10,128]{2,0,1:T(8,128)S(1)} collective-permute-done((f32[5,10,128]{2,0,1:T(8,128)S(1)}, f32[5,10,128]{2,0,1:T(8,128)S(1)}, u32[]{:S(2)}, u32[]{:S(2)}) %collective-permute-start.6) | collective-permute-done | bytes 25632 | tf_op jit(solution)/shard_map/ppermute | solution.py:48
  126.9 0.8 copy-done.3
  (263 shorter events, 8.4 us)
Async XLA Ops:
  0.6 2.0 %copy-start = (f32[19,8,8,128]{3,2,1,0:T(8,128)S(1)}, f32[19,8,8,128]{3,2,1,0:T(8,128)}, u32[]{:S(2)}) copy-start(f32[19,8,8,128]{3,2,1,0:T(8,128)} %param.3) | copy-start | bytes 1867780
  2.6 0.8 copy-start.1
  4.0 0.7 copy-start.2
  48.2 10.4 %collective-permute-start = (f32[5,8,128]{2,1,0:T(8,128)S(1)}, f32[5,8,128]{2,1,0:T(8,128)S(1)}, u32[]{:S(2)}, u32[]{:S(2)}) collective-permute-start(f32[5,8,128]{2,1,0:T(8,128)S(1)} %get-tuple-element.153), channel_id=1, source_target_pairs={{0,8},{8,16},{16,24},{1,9},{9,17},{17,25},{2,10},{10,18},{18,26},{... | collective-permute-start | bytes 61448 | tf_op jit(solution)/shard_map/ppermute | solution.py:42
  53.5 5.1 %collective-permute-start.1 = (f32[5,8,128]{2,1,0:T(8,128)S(1)}, f32[5,8,128]{2,1,0:T(8,128)S(1)}, u32[]{:S(2)}, u32[]{:S(2)}) collective-permute-start(f32[5,8,128]{2,1,0:T(8,128)S(1)} %get-tuple-element.154), channel_id=1, source_target_pairs={{8,0},{16,8},{24,16},{9,1},{17,9},{25,17},{10,2},{18,10},{26,18},{... | collective-permute-start | bytes 61448 | tf_op jit(solution)/shard_map/ppermute | solution.py:42
  58.7 5.6 %collective-permute-start.2 = (f32[5,10,128]{2,0,1:T(8,128)S(1)}, f32[5,10,128]{2,0,1:T(8,128)S(1)}, u32[]{:S(2)}, u32[]{:S(2)}) collective-permute-start(f32[5,10,128]{2,0,1:T(8,128)S(1)} %stack.145), channel_id=1, source_target_pairs={{0,1},{1,2},{2,3},{3,4},{4,5},{5,6},{6,7},{7,0},{8,9},{9,10},{10,1... | collective-permute-start | bytes 76808 | tf_op jit(solution)/shard_map/ppermute | solution.py:48
  59.2 5.2 %collective-permute-start.3 = (f32[5,10,128]{2,0,1:T(8,128)S(1)}, f32[5,10,128]{2,0,1:T(8,128)S(1)}, u32[]{:S(2)}, u32[]{:S(2)}) collective-permute-start(f32[5,10,128]{2,0,1:T(8,128)S(1)} %stack.147), channel_id=1, source_target_pairs={{0,7},{1,0},{2,1},{3,2},{4,3},{5,4},{6,5},{7,6},{8,15},{9,8},{10,9... | collective-permute-start | bytes 76808 | tf_op jit(solution)/shard_map/ppermute | solution.py:48
  108.2 7.8 %collective-permute-start.4 = (f32[5,8,128]{2,1,0:T(8,128)S(1)}, f32[5,8,128]{2,1,0:T(8,128)S(1)}, u32[]{:S(2)}, u32[]{:S(2)}) collective-permute-start(f32[5,8,128]{2,1,0:T(8,128)S(1)} %get-tuple-element.125), channel_id=1, source_target_pairs={{0,8},{8,16},{16,24},{1,9},{9,17},{17,25},{2,10},{10,18},{18,26},{... | collective-permute-start | bytes 61448 | tf_op jit(solution)/shard_map/ppermute | solution.py:42
  113.4 5.1 %collective-permute-start.5 = (f32[5,8,128]{2,1,0:T(8,128)S(1)}, f32[5,8,128]{2,1,0:T(8,128)S(1)}, u32[]{:S(2)}, u32[]{:S(2)}) collective-permute-start(f32[5,8,128]{2,1,0:T(8,128)S(1)} %get-tuple-element.124), channel_id=1, source_target_pairs={{8,0},{16,8},{24,16},{9,1},{17,9},{25,17},{10,2},{18,10},{26,18},{... | collective-permute-start | bytes 61448 | tf_op jit(solution)/shard_map/ppermute | solution.py:42
  118.7 6.9 %collective-permute-start.7 = (f32[5,10,128]{2,0,1:T(8,128)S(1)}, f32[5,10,128]{2,0,1:T(8,128)S(1)}, u32[]{:S(2)}, u32[]{:S(2)}) collective-permute-start(f32[5,10,128]{2,0,1:T(8,128)S(1)} %stack.347), channel_id=1, source_target_pairs={{0,7},{1,0},{2,1},{3,2},{4,3},{5,4},{6,5},{7,6},{8,15},{9,8},{10,9... | collective-permute-start | bytes 76808 | tf_op jit(solution)/shard_map/ppermute | solution.py:48
  119.5 5.6 %collective-permute-start.6 = (f32[5,10,128]{2,0,1:T(8,128)S(1)}, f32[5,10,128]{2,0,1:T(8,128)S(1)}, u32[]{:S(2)}, u32[]{:S(2)}) collective-permute-start(f32[5,10,128]{2,0,1:T(8,128)S(1)} %stack.172), channel_id=1, source_target_pairs={{0,1},{1,2},{2,3},{3,4},{4,5},{5,6},{6,7},{7,0},{8,9},{9,10},{10,1... | collective-permute-start | bytes 76808 | tf_op jit(solution)/shard_map/ppermute | solution.py:48
  126.9 0.8 copy-start.3
where the time goes:
time: 128 us
  blocking collectives  79.2 us (62%)
  starting transfers between devices  20.2 us (16%)
  waiting for transfers between devices  11.3 us (9%)
  other arithmetic  8.05 us (6%)
  local copies, waits for them, and re-layouts  6.31 us (5%)
  between operations  2.01 us (2%)
    psum x2, blocking collectives, outlet_mean(): totals, counts = lax.psum((local_sums, local_counts), ('gx', 'gy'))  79.2 us
    ppermute x4, starting transfers between devices, from_behind(): return lax.ppermute(block, axis, route)  14.4 us
    ppermute x4, starting transfers between devices, from_behind_2(): return lax.ppermute(value, axis, pairs)  5.84 us
    ppermute x4, waiting for transfers between devices, from_behind(): return lax.ppermute(block, axis, route)  5.67 us
    ppermute x4, waiting for transfers between devices, from_behind_2(): return lax.ppermute(value, axis, pairs)  5.62 us
    unnamed x80, other arithmetic  4.53 us
    unnamed x79, local copies, waits for them, and re-layouts  3.4 us
  transfers between devices with their start and end apart: 8, of which 4 were waited for; matrix products, arithmetic and copies ran while one was open for 1% of the time, Pallas kernels for 0%

commit v1 on v0

--- a/solution.py
+++ b/solution.py
@@ -106,7 +106,7 @@
     col_count = jnp.sum(is_outlet.astype(jnp.float32), axis=2).reshape(-1)
     local_sums = jnp.dot(onehot, column, precision=lax.Precision.HIGHEST)
     local_counts = jnp.dot(onehot, col_count, precision=lax.Precision.HIGHEST)
-    totals, counts = lax.psum((local_sums, local_counts), ("gx", "gy"))
+    totals, counts = lax.psum(lax.psum((local_sums, local_counts), "gx"), "gy")
     return totals / counts
 
 

time: 128 us -> 101 us (0.79)
  blocking collectives: 79.2 us -> 47.5 us
  starting transfers between devices: 20.2 us -> 25.1 us
    psum x2 -> x4, blocking collectives: 79.2 us -> 47.5 us  [outlet_mean(): totals, counts = lax.psum(lax.psum((local_sums, local_counts), 'gx'), 'gy')]
    ppermute x4, starting transfers between devices: 14.4 us -> 19.3 us  [from_behind(): return lax.ppermute(block, axis, route)]
  transfers between devices with their start and end apart: 8 -> 8, of which waited for: 4 -> 4; matrix products, arithmetic and copies ran while one was open for 1% -> 2% of each run, Pallas kernels for 0% -> 0%
where the time goes in v1:
time: 101 us; the launch traced here: 100 us
  blocking collectives  47.5 us (47%)
  starting transfers between devices  25.1 us (25%)
  waiting for transfers between devices  10.5 us (10%)
  other arithmetic  8.06 us (8%)
  local copies, waits for them, and re-layouts  6.31 us (6%)
  between operations  2.03 us (2%)
    psum x4, blocking collectives, outlet_mean(): totals, counts = lax.psum(lax.psum((local_sums, local_counts), 'gx'), 'gy')  47.5 us
    ppermute x4, starting transfers between devices, from_behind(): return lax.ppermute(block, axis, route)  19.3 us
    ppermute x4, starting transfers between devices, from_behind_2(): return lax.ppermute(value, axis, pairs)  5.81 us
    ppermute x4, waiting for transfers between devices, from_behind(): return lax.ppermute(block, axis, route)  5.67 us
    ppermute x4, waiting for transfers between devices, from_behind_2(): return lax.ppermute(value, axis, pairs)  4.86 us
    unnamed x80, other arithmetic  4.53 us
    unnamed x79, local copies, waits for them, and re-layouts  3.41 us
  transfers between devices with their start and end apart: 8, of which 4 were waited for; matrix products, arithmetic and copies ran while one was open for 2% of the time, Pallas kernels for 0%

profile of v1, /device:TPU:1, one launch (start us, length us, event | category | flops | bytes accessed | tf_op | source)
XLA Modules:
  0.0 100.2 jit_solution(17245517884360447215)
XLA Ops:
  0.7 0.8 constant_dynamic-update-slice_fusion.47
  1.5 1.1 %reduce_sum.854 = f32[8,8,128]{2,1,0:T(8,128)S(1)} reduce(f32[19,8,8,128]{3,2,1,0:T(8,128)} %param.3, f32[]{:T(128)} %constant.20.clone.1), dimensions={0}, to_apply=%region_0.0 | reduce | flops 147456 | bytes 655364 | tf_op jit(solution)/shard_map/reduce_sum | solution.py:103
  2.6 0.1 constant_dynamic-update-slice_fusion.66
  2.7 0.7 copy-done.1
  3.4 0.1 convert_reduce_fusion
  4.1 0.6 copy-done.2
  4.8 0.1 convolution_bitcast_fusion.3
  4.9 0.2 convolution_bitcast_fusion.4
  5.1 6.4 %all-reduce.1 = (f32[64]{0:T(128)S(1)}, f32[64]{0:T(128)S(1)}) all-reduce(f32[64]{0:T(128)S(1)} %convolution_bitcast_fusion.4, f32[64]{0:T(128)S(1)} %convolution_bitcast_fusion.3), channel_id=1, replica_groups=mesh['gx'=4,'gy'=8] {'gx'}, use_global_device_ids=true, to_apply=%region_2.3 | all-reduce | flops 128 | bytes 1024 | tf_op jit(solution)/shard_map/psum | solution.py:109
  11.5 18.0 %all-reduce = (f32[64]{0:T(128)S(1)}, f32[64]{0:T(128)S(1)}) all-reduce(f32[64]{0:T(128)S(1)} %get-tuple-element.8, f32[64]{0:T(128)S(1)} %get-tuple-element.9), channel_id=1, replica_groups=mesh['gx'=4,'gy'=8] {'gy'}, use_global_device_ids=true, to_apply=%region_3.4 | all-reduce | flops 128 | bytes 1024 | tf_op jit(solution)/shard_map/psum | solution.py:109
  29.5 0.1 broadcast_multiply_fusion.2
  31.7 0.3 select_select_fusion.1
  32.1 7.6 %collective-permute-start = (f32[5,8,128]{2,1,0:T(8,128)S(1)}, f32[5,8,128]{2,1,0:T(8,128)S(1)}, u32[]{:S(2)}, u32[]{:S(2)}) collective-permute-start(f32[5,8,128]{2,1,0:T(8,128)S(1)} %get-tuple-element.155), channel_id=1, source_target_pairs={{0,8},{8,16},{16,24},{1,9},{9,17},{17,25},{2,10},{10,18},{18,26},{... | collective-permute-start | bytes 61448 | tf_op jit(solution)/shard_map/ppermute | solution.py:42
  39.8 1.9 %collective-permute-start.1 = (f32[5,8,128]{2,1,0:T(8,128)S(1)}, f32[5,8,128]{2,1,0:T(8,128)S(1)}, u32[]{:S(2)}, u32[]{:S(2)}) collective-permute-start(f32[5,8,128]{2,1,0:T(8,128)S(1)} %get-tuple-element.156), channel_id=1, source_target_pairs={{8,0},{16,8},{24,16},{9,1},{17,9},{25,17},{10,2},{18,10},{26,18},{... | collective-permute-start | bytes 61448 | tf_op jit(solution)/shard_map/ppermute | solution.py:42
  41.8 3.1 %collective-permute-done.1 = f32[5,8,128]{2,1,0:T(8,128)S(1)} collective-permute-done((f32[5,8,128]{2,1,0:T(8,128)S(1)}, f32[5,8,128]{2,1,0:T(8,128)S(1)}, u32[]{:S(2)}, u32[]{:S(2)}) %collective-permute-start.1) | collective-permute-done | bytes 20512 | tf_op jit(solution)/shard_map/ppermute | solution.py:42
  45.3 4.2 %collective-permute-start.3 = (f32[5,10,128]{2,0,1:T(8,128)S(1)}, f32[5,10,128]{2,0,1:T(8,128)S(1)}, u32[]{:S(2)}, u32[]{:S(2)}) collective-permute-start(f32[5,10,128]{2,0,1:T(8,128)S(1)} %stack.147), channel_id=1, source_target_pairs={{0,7},{1,0},{2,1},{3,2},{4,3},{5,4},{6,5},{7,6},{8,15},{9,8},{10,9... | collective-permute-start | bytes 76808 | tf_op jit(solution)/shard_map/ppermute | solution.py:48
  49.5 1.1 %collective-permute-done.2 = f32[5,10,128]{2,0,1:T(8,128)S(1)} collective-permute-done((f32[5,10,128]{2,0,1:T(8,128)S(1)}, f32[5,10,128]{2,0,1:T(8,128)S(1)}, u32[]{:S(2)}, u32[]{:S(2)}) %collective-permute-start.2) | collective-permute-done | bytes 25632 | tf_op jit(solution)/shard_map/ppermute | solution.py:48
  52.0 0.3 constant_dynamic-update-slice_fusion.152
  53.1 0.1 fusion.168
  53.3 0.1 convolution_bitcast_fusion.1
  53.5 5.1 %psum.52 = f32[64]{0:T(128)S(1)} all-reduce(f32[64]{0:T(128)S(1)} %convolution_bitcast_fusion.1), channel_id=1, replica_groups=mesh['gx'=4,'gy'=8] {'gx'}, use_global_device_ids=true, to_apply=%region_8.9 | all-reduce | flops 64 | bytes 512 | tf_op jit(solution)/shard_map/psum | solution.py:109
  58.6 18.0 %psum.53 = f32[64]{0:T(128)S(1)} all-reduce(f32[64]{0:T(128)S(1)} %psum.52), channel_id=1, replica_groups=mesh['gx'=4,'gy'=8] {'gy'}, use_global_device_ids=true, to_apply=%region_9.10 | all-reduce | flops 64 | bytes 512 | tf_op jit(solution)/shard_map/psum | solution.py:109
  76.6 0.1 broadcast_multiply_fusion.1
  77.0 0.1 constant_dynamic-update-slice_fusion.94
  78.4 0.3 select_select_fusion
  78.9 7.8 %collective-permute-start.4 = (f32[5,8,128]{2,1,0:T(8,128)S(1)}, f32[5,8,128]{2,1,0:T(8,128)S(1)}, u32[]{:S(2)}, u32[]{:S(2)}) collective-permute-start(f32[5,8,128]{2,1,0:T(8,128)S(1)} %get-tuple-element.127), channel_id=1, source_target_pairs={{0,8},{8,16},{16,24},{1,9},{9,17},{17,25},{2,10},{10,18},{18,26},{... | collective-permute-start | bytes 61448 | tf_op jit(solution)/shard_map/ppermute | solution.py:42
  86.7 1.9 %collective-permute-start.5 = (f32[5,8,128]{2,1,0:T(8,128)S(1)}, f32[5,8,128]{2,1,0:T(8,128)S(1)}, u32[]{:S(2)}, u32[]{:S(2)}) collective-permute-start(f32[5,8,128]{2,1,0:T(8,128)S(1)} %get-tuple-element.126), channel_id=1, source_target_pairs={{8,0},{16,8},{24,16},{9,1},{17,9},{25,17},{10,2},{18,10},{26,18},{... | collective-permute-start | bytes 61448 | tf_op jit(solution)/shard_map/ppermute | solution.py:42
  88.7 0.6 pad_maximum_fusion.164
  89.3 2.6 %collective-permute-done.5 = f32[5,8,128]{2,1,0:T(8,128)S(1)} collective-permute-done((f32[5,8,128]{2,1,0:T(8,128)S(1)}, f32[5,8,128]{2,1,0:T(8,128)S(1)}, u32[]{:S(2)}, u32[]{:S(2)}) %collective-permute-start.5) | collective-permute-done | bytes 20512 | tf_op jit(solution)/shard_map/ppermute | solution.py:42
  92.1 1.5 %collective-permute-start.6 = (f32[5,10,128]{2,0,1:T(8,128)S(1)}, f32[5,10,128]{2,0,1:T(8,128)S(1)}, u32[]{:S(2)}, u32[]{:S(2)}) collective-permute-start(f32[5,10,128]{2,0,1:T(8,128)S(1)} %stack.172), channel_id=1, source_target_pairs={{0,1},{1,2},{2,3},{3,4},{4,5},{5,6},{6,7},{7,0},{8,9},{9,10},{10,1... | collective-permute-start | bytes 76808 | tf_op jit(solution)/shard_map/ppermute | solution.py:48
  93.9 3.7 %collective-permute-done.6 = f32[5,10,128]{2,0,1:T(8,128)S(1)} collective-permute-done((f32[5,10,128]{2,0,1:T(8,128)S(1)}, f32[5,10,128]{2,0,1:T(8,128)S(1)}, u32[]{:S(2)}, u32[]{:S(2)}) %collective-permute-start.6) | collective-permute-done | bytes 25632 | tf_op jit(solution)/shard_map/ppermute | solution.py:48
  99.4 0.8 copy-done.3
  (265 shorter events, 8.6 us)
Async XLA Ops:
  0.6 2.0 %copy-start = (f32[19,8,8,128]{3,2,1,0:T(8,128)S(1)}, f32[19,8,8,128]{3,2,1,0:T(8,128)}, u32[]{:S(2)}) copy-start(f32[19,8,8,128]{3,2,1,0:T(8,128)} %param.3) | copy-start | bytes 1867780
  2.6 0.8 copy-start.1
  4.0 0.7 copy-start.2
  32.1 12.8 %collective-permute-start = (f32[5,8,128]{2,1,0:T(8,128)S(1)}, f32[5,8,128]{2,1,0:T(8,128)S(1)}, u32[]{:S(2)}, u32[]{:S(2)}) collective-permute-start(f32[5,8,128]{2,1,0:T(8,128)S(1)} %get-tuple-element.155), channel_id=1, source_target_pairs={{0,8},{8,16},{16,24},{1,9},{9,17},{17,25},{2,10},{10,18},{18,26},{... | collective-permute-start | bytes 61448 | tf_op jit(solution)/shard_map/ppermute | solution.py:42
  39.8 5.1 %collective-permute-start.1 = (f32[5,8,128]{2,1,0:T(8,128)S(1)}, f32[5,8,128]{2,1,0:T(8,128)S(1)}, u32[]{:S(2)}, u32[]{:S(2)}) collective-permute-start(f32[5,8,128]{2,1,0:T(8,128)S(1)} %get-tuple-element.156), channel_id=1, source_target_pairs={{8,0},{16,8},{24,16},{9,1},{17,9},{25,17},{10,2},{18,10},{26,18},{... | collective-permute-start | bytes 61448 | tf_op jit(solution)/shard_map/ppermute | solution.py:42
  45.0 5.6 %collective-permute-start.2 = (f32[5,10,128]{2,0,1:T(8,128)S(1)}, f32[5,10,128]{2,0,1:T(8,128)S(1)}, u32[]{:S(2)}, u32[]{:S(2)}) collective-permute-start(f32[5,10,128]{2,0,1:T(8,128)S(1)} %stack.145), channel_id=1, source_target_pairs={{0,1},{1,2},{2,3},{3,4},{4,5},{5,6},{6,7},{7,0},{8,9},{9,10},{10,1... | collective-permute-start | bytes 76808 | tf_op jit(solution)/shard_map/ppermute | solution.py:48
  45.3 5.5 %collective-permute-start.3 = (f32[5,10,128]{2,0,1:T(8,128)S(1)}, f32[5,10,128]{2,0,1:T(8,128)S(1)}, u32[]{:S(2)}, u32[]{:S(2)}) collective-permute-start(f32[5,10,128]{2,0,1:T(8,128)S(1)} %stack.147), channel_id=1, source_target_pairs={{0,7},{1,0},{2,1},{3,2},{4,3},{5,4},{6,5},{7,6},{8,15},{9,8},{10,9... | collective-permute-start | bytes 76808 | tf_op jit(solution)/shard_map/ppermute | solution.py:48
  78.9 10.3 %collective-permute-start.4 = (f32[5,8,128]{2,1,0:T(8,128)S(1)}, f32[5,8,128]{2,1,0:T(8,128)S(1)}, u32[]{:S(2)}, u32[]{:S(2)}) collective-permute-start(f32[5,8,128]{2,1,0:T(8,128)S(1)} %get-tuple-element.127), channel_id=1, source_target_pairs={{0,8},{8,16},{16,24},{1,9},{9,17},{17,25},{2,10},{10,18},{18,26},{... | collective-permute-start | bytes 61448 | tf_op jit(solution)/shard_map/ppermute | solution.py:42
  86.7 5.1 %collective-permute-start.5 = (f32[5,8,128]{2,1,0:T(8,128)S(1)}, f32[5,8,128]{2,1,0:T(8,128)S(1)}, u32[]{:S(2)}, u32[]{:S(2)}) collective-permute-start(f32[5,8,128]{2,1,0:T(8,128)S(1)} %get-tuple-element.126), channel_id=1, source_target_pairs={{8,0},{16,8},{24,16},{9,1},{17,9},{25,17},{10,2},{18,10},{26,18},{... | collective-permute-start | bytes 61448 | tf_op jit(solution)/shard_map/ppermute | solution.py:42
  91.9 6.2 %collective-permute-start.7 = (f32[5,10,128]{2,0,1:T(8,128)S(1)}, f32[5,10,128]{2,0,1:T(8,128)S(1)}, u32[]{:S(2)}, u32[]{:S(2)}) collective-permute-start(f32[5,10,128]{2,0,1:T(8,128)S(1)} %stack.347), channel_id=1, source_target_pairs={{0,7},{1,0},{2,1},{3,2},{4,3},{5,4},{6,5},{7,6},{8,15},{9,8},{10,9... | collective-permute-start | bytes 76808 | tf_op jit(solution)/shard_map/ppermute | solution.py:48
  92.1 5.6 %collective-permute-start.6 = (f32[5,10,128]{2,0,1:T(8,128)S(1)}, f32[5,10,128]{2,0,1:T(8,128)S(1)}, u32[]{:S(2)}, u32[]{:S(2)}) collective-permute-start(f32[5,10,128]{2,0,1:T(8,128)S(1)} %stack.172), channel_id=1, source_target_pairs={{0,1},{1,2},{2,3},{3,4},{4,5},{5,6},{6,7},{7,0},{8,9},{9,10},{10,1... | collective-permute-start | bytes 76808 | tf_op jit(solution)/shard_map/ppermute | solution.py:48
  99.4 0.8 copy-start.3
